TPU v7x, 32 devices: a whole 2x2x4 slice. The times are simulated.
32 devices in a mesh: members: 2 (over y), comp: 4 (over z), lat: 2 (over x), sub: 2 (over core).
Axes of the slice: x: 2, y: 2, z: 4, core: 2. Of those that a mesh axis runs over, the one named last changes fastest.
Arguments:
- spectrum: float32 [1920, 4096], P('comp', ('members', 'lat', 'sub')), parts along dimension 1, may hold values from 0.05 to 2
- sea_mask: int32 [4096], P(('members', 'lat', 'sub')), parts along dimension 0, may hold values 0 or 1
- neighbours: int32 [4, 4096], P(None, ('members', 'lat', 'sub')), parts along dimension 1, may hold values from 0 to 2047, as said below
- substeps: int32 [30], replicated, may hold values from 1 to 6, as said below
- courant: float32 [30], replicated, may hold values from 0.2 to 0.7
- source_operator: bfloat16 [1920, 1920], P('sub'), may hold values from -0.125 to 0.125
Outputs:
- new_spectrum: float32 [1920, 4096], P('comp', ('members', 'lat', 'sub')), parts along dimension 1
There are 2 independent parts, one for each index of `members`. A program takes and returns all parts, laid end to end along the dimension named above; an argument that names none is the same for every part. Nothing has to cross between parts.
Inputs may be any that keep to these rules, and one draw needn't show every extreme that they name: Non-increasing with the band; the first band takes 6 substeps and the last band one. Points are numbered row by row, 256 to a row. The west and east neighbours lie in the same row, one or two columns away, wrapping around the row. The south neighbour lies in the row before and the north neighbour in the row after, within one column (wrapping); on the first and last row of the member's grid that neighbour is the point itself.
All inputs are finite; a program needn't handle non-finite values. No bound on the sum of `sea_mask` on one device may be relied on, other than what follows from the above.
Results may differ from a plain program's by a relative error of at most 0.0015.
Values may be sent and summed in bfloat16 or wider, within the bound.
A program may use at most 64 MiB of HBM per device.

v0:
```python
import math

import jax
import jax.numpy as jnp
from jax import lax
from jax.sharding import PartitionSpec as P

NF = 30
ND = 64
NLON = 256
MAXSTEPS = 6
SRC_STEPS = 4


STEP_SIZE = 0.1


def extended(cells, sides, width):
    for axis, dim in sides:
        count = lax.axis_size(axis)
        ends = count - 1
        head = lax.slice_in_dim(cells, 0, width, axis=dim)
        tail = lax.slice_in_dim(cells, cells.shape[dim] - width, cells.shape[dim], axis=dim)
        cells = jnp.concatenate(
            [
                lax.ppermute(tail, axis, [(i, (i + 1) % count) for i in range(ends)]),
                cells,
                lax.ppermute(head, axis, [((i + 1) % count, i) for i in range(ends)]),
            ],
            axis=dim,
        )
    return cells


def bin_tables(global_bins, substeps, courant):
    frequency = global_bins // ND
    direction = global_bins % ND
    chosen = frequency[:, None] == jnp.arange(NF, dtype=jnp.int32)[None, :]
    bin_steps = jnp.sum(jnp.where(chosen, substeps[None, :], 0), axis=1)
    bin_speed = jnp.sum(jnp.where(chosen, courant[None, :], 0.0), axis=1)
    angles = (direction.astype(jnp.float32) + 0.5) * (2.0 * math.pi / ND)
    cosine = jnp.cos(angles)
    sine_dir = jnp.sin(angles)
    return (
        bin_steps,
        bin_speed * jnp.abs(cosine),
        bin_speed * jnp.abs(sine_dir),
        cosine > 0,
        sine_dir > 0,
    )


def offset_codes(neighbours, sea_float, points_local):
    position = lax.axis_index(("lat", "sub")) * points_local + jnp.arange(
        points_local, dtype=jnp.int32
    )
    column = position % NLON
    west_gap = (column - neighbours[0] % NLON) % NLON
    east_gap = (neighbours[1] % NLON - column) % NLON

    def vertical_code(index_row):
        column_move = (index_row % NLON - column + 1) % NLON - 1
        return jnp.where(index_row == position, 2, column_move)

    stacked = jnp.stack(
        [west_gap, east_gap, vertical_code(neighbours[2]), vertical_code(neighbours[3])]
    ).astype(jnp.float32)
    return jnp.concatenate([stacked, sea_float[None, :]], axis=0).reshape(
        5, points_local // NLON, NLON
    )


def column_roll(values, amount):
    return jnp.roll(values, amount, axis=-1)


def vertical_pick(other_rows, code_row, center):
    moved = jnp.where(
        code_row == -1.0,
        column_roll(other_rows, 1),
        jnp.where(code_row == 1.0, column_roll(other_rows, -1), other_rows),
    )
    return jnp.where(code_row == 2.0, center, moved)


def advance(substep, center, below, above, point_codes, tables):
    bin_steps, weight_x, weight_y, from_west, from_south = tables
    west_vals = jnp.where(
        point_codes[0][None] == 1.0, column_roll(center, 1), column_roll(center, 2)
    )
    east_vals = jnp.where(
        point_codes[1][None] == 1.0, column_roll(center, -1), column_roll(center, -2)
    )
    upwind_lon = jnp.where(from_west[:, None, None], west_vals, east_vals)
    south_vals = vertical_pick(below, point_codes[2][None], center)
    north_vals = vertical_pick(above, point_codes[3][None], center)
    upwind_lat = jnp.where(from_south[:, None, None], south_vals, north_vals)
    advanced = point_codes[4][None] * (
        center
        - weight_x[:, None, None] * (center - upwind_lon)
        - weight_y[:, None, None] * (center - upwind_lat)
    )
    return jnp.where((substep < bin_steps)[:, None, None], advanced, center)


def propagate(spec_part, global_bins, substeps, courant, point_codes):
    tables = bin_tables(global_bins, substeps, courant)
    bin_count = spec_part.shape[0]
    points_local = spec_part.shape[1]
    row_count = points_local // NLON
    field_now = spec_part.reshape(bin_count, row_count, NLON)
    for substep in range(MAXSTEPS):
        padded = extended(field_now, ((("lat", "sub"), 1),), 1)
        field_now = advance(substep, field_now, padded[:, :-2], padded[:, 2:], point_codes, tables)
    return field_now.reshape(bin_count, points_local)


def per_device(spectrum, sea_mask, neighbours, substeps, courant, source_operator):
    comp_index = lax.axis_index("comp")
    bins_local = spectrum.shape[0]
    points_local = spectrum.shape[1]
    sea_float = sea_mask.astype(jnp.float32)
    point_codes = offset_codes(neighbours, sea_float, points_local)
    field_start = sea_float[None, :] * spectrum
    first_bin = comp_index * bins_local
    held_bins = first_bin + jnp.arange(bins_local, dtype=jnp.int32)
    propagated = propagate(field_start, held_bins, substeps, courant, point_codes)
    outgoing = propagated.astype(jnp.bfloat16)
    owned_cols = lax.all_to_all(outgoing, "comp", split_axis=1, concat_axis=0, tiled=True)
    whole_operator = lax.all_gather(source_operator, "sub", axis=0, tiled=True)
    point_rows = owned_cols.T
    start_state = point_rows.astype(jnp.float32)
    state_now = start_state
    full_rows = point_rows
    for source_step in range(SRC_STEPS):
        driving = lax.dot_general(
            full_rows, whole_operator, (((1,), (1,)), ((), ())), preferred_element_type=jnp.float32
        )
        state_now = state_now + STEP_SIZE * state_now * driving
        if source_step + 1 < SRC_STEPS:
            full_rows = state_now.astype(jnp.bfloat16)
    returned = (state_now - start_state).astype(jnp.bfloat16).T
    home_bins = lax.all_to_all(returned, "comp", split_axis=0, concat_axis=1, tiled=True)
    return sea_float[None, :] * (propagated + home_bins.astype(jnp.float32))


def solution(mesh):
    placed = (
        P("comp", ("members", "lat", "sub")),
        P(("members", "lat", "sub")),
        P(None, ("members", "lat", "sub")),
        P(),
        P(),
        P("sub", None),
    )
    return jax.shard_map(
        per_device,
        mesh=mesh,
        in_specs=placed,
        out_specs=P("comp", ("members", "lat", "sub")),
        check_vma=False,
    )
```

profile of v0, /device:TPU:2, one launch (start us, length us, event | category | flops | bytes accessed | tf_op | source)
XLA Modules:
  0.0 158.7 jit_solution(9278967915208655400)
XLA Ops:
  9.0 1.9 %collective-permute-start.1 = (f32[480,1,256]{0,2,1:T(8,128)S(1)}, f32[480,1,256]{0,2,1:T(8,128)S(1)}, u32[]{:S(2)}, u32[]{:S(2)}) collective-permute-start(f32[480,1,256]{0,2,1:T(8,128)S(1)} %get-tuple-element.124), channel_id=1, source_target_pairs={{1,0},{2,1},{3,2},{5,4},{6,5},{7,6},{9,8},{10,9},{11,10},{13,12},{... | collective-permute-start | bytes 1474568 | tf_op jit(solution)/shard_map/ppermute | solution.py:28
  10.9 2.6 %collective-permute-start = (f32[480,1,256]{0,2,1:T(8,128)S(1)}, f32[480,1,256]{0,2,1:T(8,128)S(1)}, u32[]{:S(2)}, u32[]{:S(2)}) collective-permute-start(f32[480,1,256]{0,2,1:T(8,128)S(1)} %get-tuple-element.123), channel_id=1, source_target_pairs={{0,1},{1,2},{2,3},{4,5},{5,6},{6,7},{8,9},{9,10},{10,11},{12,13},{... | collective-permute-start | bytes 1474568 | tf_op jit(solution)/shard_map/ppermute | solution.py:26
  14.5 3.1 %collective-permute-done.1 = f32[480,1,256]{0,2,1:T(8,128)S(1)} collective-permute-done((f32[480,1,256]{0,2,1:T(8,128)S(1)}, f32[480,1,256]{0,2,1:T(8,128)S(1)}, u32[]{:S(2)}, u32[]{:S(2)}) %collective-permute-start.1) | collective-permute-done | bytes 491552 | tf_op jit(solution)/shard_map/ppermute | solution.py:28
  17.6 4.0 %collective-permute-done = f32[480,1,256]{0,2,1:T(8,128)S(1)} collective-permute-done((f32[480,1,256]{0,2,1:T(8,128)S(1)}, f32[480,1,256]{0,2,1:T(8,128)S(1)}, u32[]{:S(2)}, u32[]{:S(2)}) %collective-permute-start) | collective-permute-done | bytes 491552 | tf_op jit(solution)/shard_map/ppermute | solution.py:26
  22.4 3.3 %fusion.108 = f32[480,2,256]{0,2,1:T(8,128)S(1)} fusion(f32[480,2,256]{0,2,1:T(8,128)S(1)} %bitcast.72, f32[480,1,256]{0,2,1:T(8,128)S(1)} %collective-permute-done.1, f32[480,1,256]{0,2,1:T(8,128)S(1)} %collective-permute-done, f32[480,2,255]{0,2,1:T(8,128)S(1)} %get-tuple-element.112, f32[480,2,1]{0,2,1:T(1,128)S(1)} %get-tuple-element.118, ...), kind=kLoop, calls=%fused_computation.205 | loop fusion | flops 7372800 | bytes 10817184 | tf_op jit(solution)/shard_map/jit(_where)/select_n | solution.py:103
  27.7 2.4 %collective-permute-start.2 = (f32[480,1,256]{0,2,1:T(8,128)S(1)}, f32[480,1,256]{0,2,1:T(8,128)S(1)}, u32[]{:S(2)}, u32[]{:S(2)}) collective-permute-start(f32[480,1,256]{0,2,1:T(8,128)S(1)} %get-tuple-element.109), channel_id=1, source_target_pairs={{0,1},{1,2},{2,3},{4,5},{5,6},{6,7},{8,9},{9,10},{10,11},{12,13},{... | collective-permute-start | bytes 1474568 | tf_op jit(solution)/shard_map/ppermute | solution.py:26
  30.4 4.0 %collective-permute-done.3 = f32[480,1,256]{0,2,1:T(8,128)S(1)} collective-permute-done((f32[480,1,256]{0,2,1:T(8,128)S(1)}, f32[480,1,256]{0,2,1:T(8,128)S(1)}, u32[]{:S(2)}, u32[]{:S(2)}) %collective-permute-start.3) | collective-permute-done | bytes 491552 | tf_op jit(solution)/shard_map/ppermute | solution.py:28
  34.3 3.8 %collective-permute-done.2 = f32[480,1,256]{0,2,1:T(8,128)S(1)} collective-permute-done((f32[480,1,256]{0,2,1:T(8,128)S(1)}, f32[480,1,256]{0,2,1:T(8,128)S(1)}, u32[]{:S(2)}, u32[]{:S(2)}) %collective-permute-start.2) | collective-permute-done | bytes 491552 | tf_op jit(solution)/shard_map/ppermute | solution.py:26
  39.0 3.3 %fusion.94 = f32[480,2,256]{0,2,1:T(8,128)S(1)} fusion(f32[480,2,256]{0,2,1:T(8,128)S(1)} %fusion.108, f32[480,1,256]{0,2,1:T(8,128)S(1)} %collective-permute-done.3, f32[480,1,256]{0,2,1:T(8,128)S(1)} %collective-permute-done.2, f32[480,2,255]{0,2,1:T(8,128)S(1)} %get-tuple-element.100, f32[480,2,1]{0,2,1:T(1,128)S(1)} %get-tuple-element.104, ...), kind=kLoop, calls=%fused_computation.187 | loop fusion | flops 7372800 | bytes 10817184 | tf_op jit(solution)/shard_map/jit(_where)/select_n | solution.py:103
  44.3 2.4 %collective-permute-start.4 = (f32[480,1,256]{0,2,1:T(8,128)S(1)}, f32[480,1,256]{0,2,1:T(8,128)S(1)}, u32[]{:S(2)}, u32[]{:S(2)}) collective-permute-start(f32[480,1,256]{0,2,1:T(8,128)S(1)} %get-tuple-element.95), channel_id=1, source_target_pairs={{0,1},{1,2},{2,3},{4,5},{5,6},{6,7},{8,9},{9,10},{10,11},{12,13},{... | collective-permute-start | bytes 1474568 | tf_op jit(solution)/shard_map/ppermute | solution.py:26
  47.0 4.0 %collective-permute-done.5 = f32[480,1,256]{0,2,1:T(8,128)S(1)} collective-permute-done((f32[480,1,256]{0,2,1:T(8,128)S(1)}, f32[480,1,256]{0,2,1:T(8,128)S(1)}, u32[]{:S(2)}, u32[]{:S(2)}) %collective-permute-start.5) | collective-permute-done | bytes 491552 | tf_op jit(solution)/shard_map/ppermute | solution.py:28
  51.0 3.8 %collective-permute-done.4 = f32[480,1,256]{0,2,1:T(8,128)S(1)} collective-permute-done((f32[480,1,256]{0,2,1:T(8,128)S(1)}, f32[480,1,256]{0,2,1:T(8,128)S(1)}, u32[]{:S(2)}, u32[]{:S(2)}) %collective-permute-start.4) | collective-permute-done | bytes 491552 | tf_op jit(solution)/shard_map/ppermute | solution.py:26
  55.7 3.3 %fusion.80 = f32[480,2,256]{0,2,1:T(8,128)S(1)} fusion(f32[480,2,256]{0,2,1:T(8,128)S(1)} %fusion.94, f32[480,1,256]{0,2,1:T(8,128)S(1)} %collective-permute-done.5, f32[480,1,256]{0,2,1:T(8,128)S(1)} %collective-permute-done.4, f32[480,2,255]{0,2,1:T(8,128)S(1)} %get-tuple-element.86, f32[480,2,1]{0,2,1:T(1,128)S(1)} %get-tuple-element.90, ...), kind=kLoop, calls=%fused_computation.169 | loop fusion | flops 7372800 | bytes 10817184 | tf_op jit(solution)/shard_map/jit(_where)/select_n | solution.py:103
  61.0 2.4 %collective-permute-start.6 = (f32[480,1,256]{0,2,1:T(8,128)S(1)}, f32[480,1,256]{0,2,1:T(8,128)S(1)}, u32[]{:S(2)}, u32[]{:S(2)}) collective-permute-start(f32[480,1,256]{0,2,1:T(8,128)S(1)} %get-tuple-element.81), channel_id=1, source_target_pairs={{0,1},{1,2},{2,3},{4,5},{5,6},{6,7},{8,9},{9,10},{10,11},{12,13},{... | collective-permute-start | bytes 1474568 | tf_op jit(solution)/shard_map/ppermute | solution.py:26
  63.7 4.0 %collective-permute-done.7 = f32[480,1,256]{0,2,1:T(8,128)S(1)} collective-permute-done((f32[480,1,256]{0,2,1:T(8,128)S(1)}, f32[480,1,256]{0,2,1:T(8,128)S(1)}, u32[]{:S(2)}, u32[]{:S(2)}) %collective-permute-start.7) | collective-permute-done | bytes 491552 | tf_op jit(solution)/shard_map/ppermute | solution.py:28
  67.7 3.8 %collective-permute-done.6 = f32[480,1,256]{0,2,1:T(8,128)S(1)} collective-permute-done((f32[480,1,256]{0,2,1:T(8,128)S(1)}, f32[480,1,256]{0,2,1:T(8,128)S(1)}, u32[]{:S(2)}, u32[]{:S(2)}) %collective-permute-start.6) | collective-permute-done | bytes 491552 | tf_op jit(solution)/shard_map/ppermute | solution.py:26
  72.3 3.3 %fusion.66 = f32[480,2,256]{0,2,1:T(8,128)S(1)} fusion(f32[480,2,256]{0,2,1:T(8,128)S(1)} %fusion.80, f32[480,1,256]{0,2,1:T(8,128)S(1)} %collective-permute-done.7, f32[480,1,256]{0,2,1:T(8,128)S(1)} %collective-permute-done.6, f32[480,2,255]{0,2,1:T(8,128)S(1)} %get-tuple-element.72, f32[480,2,1]{0,2,1:T(1,128)S(1)} %get-tuple-element.76, ...), kind=kLoop, calls=%fused_computation.151 | loop fusion | flops 7372800 | bytes 10817184 | tf_op jit(solution)/shard_map/jit(_where)/select_n | solution.py:103
  77.7 2.4 %collective-permute-start.8 = (f32[480,1,256]{0,2,1:T(8,128)S(1)}, f32[480,1,256]{0,2,1:T(8,128)S(1)}, u32[]{:S(2)}, u32[]{:S(2)}) collective-permute-start(f32[480,1,256]{0,2,1:T(8,128)S(1)} %get-tuple-element.67), channel_id=1, source_target_pairs={{0,1},{1,2},{2,3},{4,5},{5,6},{6,7},{8,9},{9,10},{10,11},{12,13},{... | collective-permute-start | bytes 1474568 | tf_op jit(solution)/shard_map/ppermute | solution.py:26
  80.4 4.0 %collective-permute-done.9 = f32[480,1,256]{0,2,1:T(8,128)S(1)} collective-permute-done((f32[480,1,256]{0,2,1:T(8,128)S(1)}, f32[480,1,256]{0,2,1:T(8,128)S(1)}, u32[]{:S(2)}, u32[]{:S(2)}) %collective-permute-start.9) | collective-permute-done | bytes 491552 | tf_op jit(solution)/shard_map/ppermute | solution.py:28
  84.3 3.8 %collective-permute-done.8 = f32[480,1,256]{0,2,1:T(8,128)S(1)} collective-permute-done((f32[480,1,256]{0,2,1:T(8,128)S(1)}, f32[480,1,256]{0,2,1:T(8,128)S(1)}, u32[]{:S(2)}, u32[]{:S(2)}) %collective-permute-start.8) | collective-permute-done | bytes 491552 | tf_op jit(solution)/shard_map/ppermute | solution.py:26
  89.0 3.3 %fusion.52 = f32[480,2,256]{0,2,1:T(8,128)S(1)} fusion(f32[480,2,256]{0,2,1:T(8,128)S(1)} %fusion.66, f32[480,1,256]{0,2,1:T(8,128)S(1)} %collective-permute-done.9, f32[480,1,256]{0,2,1:T(8,128)S(1)} %collective-permute-done.8, f32[480,2,255]{0,2,1:T(8,128)S(1)} %get-tuple-element.58, f32[480,2,1]{0,2,1:T(1,128)S(1)} %get-tuple-element.62, ...), kind=kLoop, calls=%fused_computation.133 | loop fusion | flops 7372800 | bytes 10817184 | tf_op jit(solution)/shard_map/jit(_where)/select_n | solution.py:103
  94.3 2.6 %collective-permute-start.10 = (f32[480,1,256]{0,2,1:T(8,128)S(1)}, f32[480,1,256]{0,2,1:T(8,128)S(1)}, u32[]{:S(2)}, u32[]{:S(2)}) collective-permute-start(f32[480,1,256]{0,2,1:T(8,128)S(1)} %get-tuple-element.53), channel_id=1, source_target_pairs={{0,1},{1,2},{2,3},{4,5},{5,6},{6,7},{8,9},{9,10},{10,11},{12,13},{... | collective-permute-start | bytes 1474568 | tf_op jit(solution)/shard_map/ppermute | solution.py:26
  97.2 3.8 %collective-permute-done.11 = f32[480,1,256]{0,2,1:T(8,128)S(1)} collective-permute-done((f32[480,1,256]{0,2,1:T(8,128)S(1)}, f32[480,1,256]{0,2,1:T(8,128)S(1)}, u32[]{:S(2)}, u32[]{:S(2)}) %collective-permute-start.11) | collective-permute-done | bytes 491552 | tf_op jit(solution)/shard_map/ppermute | solution.py:28
  101.0 3.8 %collective-permute-done.10 = f32[480,1,256]{0,2,1:T(8,128)S(1)} collective-permute-done((f32[480,1,256]{0,2,1:T(8,128)S(1)}, f32[480,1,256]{0,2,1:T(8,128)S(1)}, u32[]{:S(2)}, u32[]{:S(2)}) %collective-permute-start.10) | collective-permute-done | bytes 491552 | tf_op jit(solution)/shard_map/ppermute | solution.py:26
  105.6 3.4 %fusion.188 = (bf16[480,2,256]{0,2,1:T(8,128)(2,1)S(1)}, f32[480,2,256]{0,2,1:T(8,128)S(1)}) fusion(f32[480,2,256]{0,2,1:T(8,128)S(1)} %fusion.52, f32[480,1,256]{0,2,1:T(8,128)S(1)} %collective-permute-done.11, f32[480,2,1]{0,2,1:T(1,128)S(1)} %get-tuple-element.40, f32[480,2,255]{0,2,1:T(8,128)S(1)} %get-tuple-element.51, pred[2,256]{1,0:T(4,128)(4,1)S(1)} %eq.181, ...), kind=kLoop, calls=%fused_computation.365 | loop fusion | flops 7618560 | bytes 11308704 | tf_op jit(solution)/shard_map/convert_element_type | solution.py:128
  109.3 14.6 %all_to_all.29 = bf16[480,4,128]{2,0,1:T(8,128)(2,1)S(1)} all-to-all(bf16[480,4,128]{2,0,1:T(8,128)(2,1)S(1)} %copy.95), channel_id=1, replica_groups=mesh['members'=2,'comp'=4,'lat'=2,'sub'=2] {'comp'}, dimensions={1} | all-to-all | bytes 983040 | tf_op jit(solution)/shard_map/all_to_all | solution.py:129
  124.2 5.5 %fusion.209 = f32[128,1920]{1,0:T(8,128)S(1)} fusion(bf16[1920,128]{1,0:T(8,128)(2,1)S(1)} %bitcast.74, bf16[1920,1920]{1,0:T(8,128)(2,1)} %all-gather.2.cloned.1.call-done), kind=kOutput, calls=%fused_computation.385 | convolution fusion | flops 943718400 | bytes 8847360 | tf_op jit(solution)/shard_map/dot_general | solution.py:136
  129.7 2.2 %fusion.144 = f32[128,1920]{1,0:T(8,128)S(1)} fusion(bf16[1920,1920]{1,0:T(8,128)(2,1)S(1)} %copy-done, f32[128,1920]{1,0:T(8,128)S(1)} %fusion.209, bf16[1920,128]{0,1:T(8,128)(2,1)S(1)} %copy.96), kind=kOutput, calls=%fused_computation.262 | convolution fusion | flops 944947200 | bytes 9830400 | tf_op jit(solution)/shard_map/dot_general | solution.py:136
  132.0 2.2 %fusion.146 = f32[128,1920]{1,0:T(8,128)S(1)} fusion(bf16[1920,1920]{1,0:T(8,128)(2,1)S(1)} %copy-done, f32[128,1920]{1,0:T(8,128)S(1)} %fusion.144, f32[128,1920]{1,0:T(8,128)S(1)} %fusion.209, bf16[1920,128]{0,1:T(8,128)(2,1)S(1)} %copy.96), kind=kOutput, calls=%fused_computation.263 | convolution fusion | flops 945684480 | bytes 10813440 | tf_op jit(solution)/shard_map/dot_general | solution.py:136
  134.2 2.2 %fusion.3 = bf16[1920,128]{0,1:T(8,128)(2,1)S(1)} fusion(bf16[1920,1920]{1,0:T(8,128)(2,1)S(1)} %copy-done, bf16[1920,128]{0,1:T(8,128)(2,1)S(1)} %copy.96, f32[128,1920]{1,0:T(8,128)S(1)} %fusion.146, f32[128,1920]{1,0:T(8,128)S(1)} %fusion.144, f32[128,1920]{1,0:T(8,128)S(1)} %fusion.209), kind=kOutput, calls=%fused_computation.40 | convolution fusion | flops 950108160 | bytes 11304960 | tf_op jit(solution)/shard_map/dot_general | solution.py:136
  137.4 3.5 %all-to-all-start.1 = ((bf16[4,480,128]{2,1,0:T(8,128)(2,1)}), bf16[4,480,128]{2,1,0:T(8,128)(2,1)S(1)}, u32[]{:S(2)}, u32[]{:S(2)}) async-start(bf16[4,480,128]{2,1,0:T(8,128)(2,1)} %bitcast.10), calls=%async_computation.1 | async-start | bytes 983040 | tf_op jit(solution)/shard_map/all_to_all | solution.py:143
  141.2 9.6 %all-to-all-done.1 = bf16[4,480,128]{2,1,0:T(8,128)(2,1)S(1)} async-done(((bf16[4,480,128]{2,1,0:T(8,128)(2,1)}), bf16[4,480,128]{2,1,0:T(8,128)(2,1)S(1)}, u32[]{:S(2)}, u32[]{:S(2)}) %all-to-all-start.1) | async-done | bytes 491552 | tf_op jit(solution)/shard_map/all_to_all | solution.py:143
  (72 shorter events, 22.2 us)
Async XLA Ops:
  6.5 117.7 %all-gather.2.cloned.1.call-start = ((), (), s32[]{:S(2)}) async-start(), calls=%async_computation.2 | async-start | bytes 11059200 | tf_op jit(solution)/shard_map/all_gather | solution.py:130
  9.0 8.6 %collective-permute-start.1 = (f32[480,1,256]{0,2,1:T(8,128)S(1)}, f32[480,1,256]{0,2,1:T(8,128)S(1)}, u32[]{:S(2)}, u32[]{:S(2)}) collective-permute-start(f32[480,1,256]{0,2,1:T(8,128)S(1)} %get-tuple-element.124), channel_id=1, source_target_pairs={{1,0},{2,1},{3,2},{5,4},{6,5},{7,6},{9,8},{10,9},{11,10},{13,12},{... | collective-permute-start | bytes 1474568 | tf_op jit(solution)/shard_map/ppermute | solution.py:28
  10.9 2.7 %copy-start.2 = (f32[30]{0:T(128)S(1)}, f32[30]{0:T(128)}, u32[]{:S(2)}) copy-start(f32[30]{0:T(128)} %param.10) | copy-start | bytes 364
  10.9 2.9 %copy-start.1 = (s32[4,512]{1,0:T(4,128)S(1)}, s32[4,512]{1,0:T(4,128)}, u32[]{:S(2)}) copy-start(s32[4,512]{1,0:T(4,128)} %param.8) | copy-start | bytes 24580
  10.9 3.2 %copy-start.3 = (s32[30]{0:T(128)S(1)}, s32[30]{0:T(128)}, u32[]{:S(2)}) copy-start(s32[30]{0:T(128)} %param.9) | copy-start | bytes 364
  10.9 10.6 %collective-permute-start = (f32[480,1,256]{0,2,1:T(8,128)S(1)}, f32[480,1,256]{0,2,1:T(8,128)S(1)}, u32[]{:S(2)}, u32[]{:S(2)}) collective-permute-start(f32[480,1,256]{0,2,1:T(8,128)S(1)} %get-tuple-element.123), channel_id=1, source_target_pairs={{0,1},{1,2},{2,3},{4,5},{5,6},{6,7},{8,9},{9,10},{10,11},{12,13},{... | collective-permute-start | bytes 1474568 | tf_op jit(solution)/shard_map/ppermute | solution.py:26
  25.7 8.6 %collective-permute-start.3 = (f32[480,1,256]{0,2,1:T(8,128)S(1)}, f32[480,1,256]{0,2,1:T(8,128)S(1)}, u32[]{:S(2)}, u32[]{:S(2)}) collective-permute-start(f32[480,1,256]{0,2,1:T(8,128)S(1)} %get-tuple-element.110), channel_id=1, source_target_pairs={{1,0},{2,1},{3,2},{5,4},{6,5},{7,6},{9,8},{10,9},{11,10},{13,12},{... | collective-permute-start | bytes 1474568 | tf_op jit(solution)/shard_map/ppermute | solution.py:28
  27.7 10.5 %collective-permute-start.2 = (f32[480,1,256]{0,2,1:T(8,128)S(1)}, f32[480,1,256]{0,2,1:T(8,128)S(1)}, u32[]{:S(2)}, u32[]{:S(2)}) collective-permute-start(f32[480,1,256]{0,2,1:T(8,128)S(1)} %get-tuple-element.109), channel_id=1, source_target_pairs={{0,1},{1,2},{2,3},{4,5},{5,6},{6,7},{8,9},{9,10},{10,11},{12,13},{... | collective-permute-start | bytes 1474568 | tf_op jit(solution)/shard_map/ppermute | solution.py:26
  42.4 8.6 %collective-permute-start.5 = (f32[480,1,256]{0,2,1:T(8,128)S(1)}, f32[480,1,256]{0,2,1:T(8,128)S(1)}, u32[]{:S(2)}, u32[]{:S(2)}) collective-permute-start(f32[480,1,256]{0,2,1:T(8,128)S(1)} %get-tuple-element.96), channel_id=1, source_target_pairs={{1,0},{2,1},{3,2},{5,4},{6,5},{7,6},{9,8},{10,9},{11,10},{13,12},{... | collective-permute-start | bytes 1474568 | tf_op jit(solution)/shard_map/ppermute | solution.py:28
  44.3 10.5 %collective-permute-start.4 = (f32[480,1,256]{0,2,1:T(8,128)S(1)}, f32[480,1,256]{0,2,1:T(8,128)S(1)}, u32[]{:S(2)}, u32[]{:S(2)}) collective-permute-start(f32[480,1,256]{0,2,1:T(8,128)S(1)} %get-tuple-element.95), channel_id=1, source_target_pairs={{0,1},{1,2},{2,3},{4,5},{5,6},{6,7},{8,9},{9,10},{10,11},{12,13},{... | collective-permute-start | bytes 1474568 | tf_op jit(solution)/shard_map/ppermute | solution.py:26
  59.1 8.6 %collective-permute-start.7 = (f32[480,1,256]{0,2,1:T(8,128)S(1)}, f32[480,1,256]{0,2,1:T(8,128)S(1)}, u32[]{:S(2)}, u32[]{:S(2)}) collective-permute-start(f32[480,1,256]{0,2,1:T(8,128)S(1)} %get-tuple-element.82), channel_id=1, source_target_pairs={{1,0},{2,1},{3,2},{5,4},{6,5},{7,6},{9,8},{10,9},{11,10},{13,12},{... | collective-permute-start | bytes 1474568 | tf_op jit(solution)/shard_map/ppermute | solution.py:28
  61.0 10.5 %collective-permute-start.6 = (f32[480,1,256]{0,2,1:T(8,128)S(1)}, f32[480,1,256]{0,2,1:T(8,128)S(1)}, u32[]{:S(2)}, u32[]{:S(2)}) collective-permute-start(f32[480,1,256]{0,2,1:T(8,128)S(1)} %get-tuple-element.81), channel_id=1, source_target_pairs={{0,1},{1,2},{2,3},{4,5},{5,6},{6,7},{8,9},{9,10},{10,11},{12,13},{... | collective-permute-start | bytes 1474568 | tf_op jit(solution)/shard_map/ppermute | solution.py:26
  75.7 8.6 %collective-permute-start.9 = (f32[480,1,256]{0,2,1:T(8,128)S(1)}, f32[480,1,256]{0,2,1:T(8,128)S(1)}, u32[]{:S(2)}, u32[]{:S(2)}) collective-permute-start(f32[480,1,256]{0,2,1:T(8,128)S(1)} %get-tuple-element.68), channel_id=1, source_target_pairs={{1,0},{2,1},{3,2},{5,4},{6,5},{7,6},{9,8},{10,9},{11,10},{13,12},{... | collective-permute-start | bytes 1474568 | tf_op jit(solution)/shard_map/ppermute | solution.py:28
  77.7 10.5 %collective-permute-start.8 = (f32[480,1,256]{0,2,1:T(8,128)S(1)}, f32[480,1,256]{0,2,1:T(8,128)S(1)}, u32[]{:S(2)}, u32[]{:S(2)}) collective-permute-start(f32[480,1,256]{0,2,1:T(8,128)S(1)} %get-tuple-element.67), channel_id=1, source_target_pairs={{0,1},{1,2},{2,3},{4,5},{5,6},{6,7},{8,9},{9,10},{10,11},{12,13},{... | collective-permute-start | bytes 1474568 | tf_op jit(solution)/shard_map/ppermute | solution.py:26
  92.4 8.6 %collective-permute-start.11 = (f32[480,1,256]{0,2,1:T(8,128)S(1)}, f32[480,1,256]{0,2,1:T(8,128)S(1)}, u32[]{:S(2)}, u32[]{:S(2)}) collective-permute-start(f32[480,1,256]{0,2,1:T(8,128)S(1)} %get-tuple-element.54), channel_id=1, source_target_pairs={{1,0},{2,1},{3,2},{5,4},{6,5},{7,6},{9,8},{10,9},{11,10},{13,12},{... | collective-permute-start | bytes 1474568 | tf_op jit(solution)/shard_map/ppermute | solution.py:28
  94.3 10.5 %collective-permute-start.10 = (f32[480,1,256]{0,2,1:T(8,128)S(1)}, f32[480,1,256]{0,2,1:T(8,128)S(1)}, u32[]{:S(2)}, u32[]{:S(2)}) collective-permute-start(f32[480,1,256]{0,2,1:T(8,128)S(1)} %get-tuple-element.53), channel_id=1, source_target_pairs={{0,1},{1,2},{2,3},{4,5},{5,6},{6,7},{8,9},{9,10},{10,11},{12,13},{... | collective-permute-start | bytes 1474568 | tf_op jit(solution)/shard_map/ppermute | solution.py:26
  124.2 5.5 %copy-start = (bf16[1920,1920]{1,0:T(8,128)(2,1)S(1)}, bf16[1920,1920]{1,0:T(8,128)(2,1)}, u32[]{:S(2)}) copy-start(bf16[1920,1920]{1,0:T(8,128)(2,1)} %all-gather.2.cloned.1.call-done) | copy-start | bytes 22118404
  137.4 13.4 %all-to-all-start.1 = ((bf16[4,480,128]{2,1,0:T(8,128)(2,1)}), bf16[4,480,128]{2,1,0:T(8,128)(2,1)S(1)}, u32[]{:S(2)}, u32[]{:S(2)}) async-start(bf16[4,480,128]{2,1,0:T(8,128)(2,1)} %bitcast.10), calls=%async_computation.1 | async-start | bytes 983040 | tf_op jit(solution)/shard_map/all_to_all | solution.py:143
Sparse Core Ops, SparseCore 0:
  13.7 20.5 all-gather.1
where the time goes:
time: 159 us
  waiting for transfers between devices  55.5 us (35%)
  starting transfers between devices  29.9 us (19%)
  other arithmetic  28.4 us (18%)
  blocking collectives  14.6 us (9%)
  between operations  13.9 us (9%)
  matrix products  12.2 us (8%)
  local copies, waits for them, and re-layouts  4.18 us (3%)
    ppermute x6, waiting for transfers between devices, extended(): lax.ppermute(tail, axis, [(i, (i + 1) % count) for i in range(ends)])  23.1 us
    ppermute x6, waiting for transfers between devices, extended(): lax.ppermute(head, axis, [((i + 1) % count, i) for i in range(ends)])  22.8 us
    select_n x5, other arithmetic, advance(): return jnp.where((substep < bin_steps)[:, None, None], advanced, center)  16.6 us
    ppermute x6, starting transfers between devices, extended(): lax.ppermute(tail, axis, [(i, (i + 1) % count) for i in range(ends)])  14.9 us
    all_to_all x1, blocking collectives, per_device(): lax.all_to_all(outgoing, 'comp', split_axis=1, concat_axis=0, tiled=True)  14.6 us
    dot_general x4, matrix products, per_device(): lax.dot_general(full_rows, whole_operator, (((1,), (1,)), ((), ())), pref...  12.2 us
    ppermute x6, starting transfers between devices, extended(): lax.ppermute(head, axis, [((i + 1) % count, i) for i in range(ends)])  11.5 us
    all_to_all x1, waiting for transfers between devices, per_device(): lax.all_to_all(returned, 'comp', split_axis=0, concat_axis=1, tiled=True)  9.57 us
  transfers between devices with their start and end apart: 14, of which 13 were waited for; matrix products, arithmetic and copies ran while one was open for 18% of the time, Pallas kernels for 0%

commit v1 on v0

v1 whole, which is shorter than its diff:
```python
import functools
import math

import jax
import jax.numpy as jnp
import numpy as np
from jax import lax
from jax.experimental import pallas as pl
from jax.experimental.pallas import tpu as pltpu
from jax.sharding import PartitionSpec as P

NF = 30
ND = 64
NLON = 256
MAXSTEPS = 6
SRC_STEPS = 4
STEP_SIZE = 0.1
MESH = pl.DeviceIdType.MESH
HALF = ND // 2
TILES = 4
SLOTS = 8
F32 = jnp.float32
BF16 = jnp.bfloat16


def kernel(
    nlat, ncomp, group, spec_ref, mask_ref, nb_ref, steps_ref, cour_ref, cos_ref, sin_ref, op_ref,
    out_ref, w_ref, own_ref, halo_ref, code_ref, prop_ref, away_ref, got_ref, start_ref, state_ref,
    low_ref, inc_ref, home_ref,
    h_send, h_recv, w_send, w_recv, w_local, a_send, a_recv, b_send, b_recv,
):
    lat = lax.axis_index("lat")
    sub = lax.axis_index("sub")
    me = lax.axis_index("comp")
    bins, points = spec_ref.shape
    chunks, size = prop_ref.shape[0], prop_ref.shape[1]
    planes = size // 8
    share = points // ncomp
    total = bins * ncomp
    half_rows = total // 2
    first = me * bins
    last_lat = nlat - 1
    partner = {"sub": 1 - sub}

    barrier = pltpu.get_barrier_semaphore()
    peers = [partner]
    if nlat == 2:
        peers.append({"lat": 1 - lat})
    else:
        for move in (1, -1):
            peers.append({"lat": lax.rem(lat + move + nlat, nlat)})
            peers.append({"lat": lax.rem(lat + 2 * move + nlat, nlat), "sub": 1 - sub})
    for j in range(1, ncomp):
        peers.append({"comp": lax.rem(me + j, ncomp)})
    for peer in peers:
        pl.semaphore_signal(barrier, inc=1, device_id=peer, device_id_type=MESH)

    own_half = pl.ds(pl.multiple_of(sub * half_rows, 16), half_rows)
    load_w = pltpu.make_async_copy(op_ref, w_ref.at[own_half], w_local)
    load_w.start()

    lane = lax.broadcasted_iota(jnp.int32, (1, points), 1)
    column = lane & (NLON - 1)
    position = (lat * 2 + sub) * points + lane
    sea = mask_ref[...].astype(F32)
    west = (column - nb_ref[0:1, :]) & (NLON - 1)
    east = (nb_ref[1:2, :] - column) & (NLON - 1)

    def vertical(index_row):
        moved = ((index_row - column + 1) & (NLON - 1)) - 1
        return jnp.where(index_row == position, 2, moved)

    rows = lax.broadcasted_iota(jnp.int32, (size, points), 0)
    codes = jnp.zeros((size, points), F32)
    entries = [west, east, vertical(nb_ref[2:3, :]), vertical(nb_ref[3:4, :])]
    for k, entry in enumerate([e.astype(F32) for e in entries] + [sea]):
        codes = jnp.where(rows == k, jnp.broadcast_to(entry, (size, points)), codes)
    own_ref[0] = codes.astype(BF16)
    own_ref[1] = codes.astype(BF16)

    pl.semaphore_wait(barrier, len(peers))

    def kind(q):
        return lax.rem(lax.div(first + (q - 2) * size, HALF), 2)

    def has_from(ty, far):
        return jnp.where(ty == 0, lat >= far, lat <= last_lat - far)

    def has_to(ty, far):
        return jnp.where(ty == 0, lat <= last_lat - far, lat >= far)

    def pair_copy(q):
        return pltpu.make_async_remote_copy(
            src_ref=own_ref.at[q], dst_ref=halo_ref.at[0, q], send_sem=h_send.at[0, q],
            recv_sem=h_recv.at[0, q], device_id=partner, device_id_type=MESH)

    def side_copy(q, ty):
        to = jnp.clip(lat + 1 - 2 * ty, 0, last_lat)
        return pltpu.make_async_remote_copy(
            src_ref=own_ref.at[q], dst_ref=halo_ref.at[1, q], send_sem=h_send.at[1, q],
            recv_sem=h_recv.at[1, q], device_id={"lat": to}, device_id_type=MESH)

    def hand_copy(q, ty):
        slot = jnp.where(sub == ty, 2, 0)
        return pltpu.make_async_remote_copy(
            src_ref=halo_ref.at[1, q], dst_ref=halo_ref.at[slot, q], send_sem=h_send.at[2, q],
            recv_sem=h_recv.at[2, q], device_id=partner, device_id_type=MESH)

    def far_copy(q, ty):
        to = jnp.clip(lat + 2 - 4 * ty, 0, last_lat)
        return pltpu.make_async_remote_copy(
            src_ref=own_ref.at[q], dst_ref=halo_ref.at[2, q], send_sem=h_send.at[3, q],
            recv_sem=h_recv.at[3, q], device_id={"lat": to, "sub": 1 - sub}, device_id_type=MESH)

    def send_own(q, ty):
        @pl.when(has_to(ty, 1))
        def _():
            side_copy(q, ty).start()

        @pl.when(sub == ty)
        def _():
            pair_copy(q).start()

        if nlat > 2:
            @pl.when((sub != ty) & has_to(ty, 2))
            def _():
                far_copy(q, ty).start()

    def hand_on(q, ty):
        @pl.when(has_from(ty, 1))
        def _():
            side_copy(q, ty).wait_recv()
            hand_copy(q, ty).start()

    def arrive(q, ty):
        @pl.when(has_from(ty, 1))
        def _():
            hand_copy(q, ty).wait_recv()

        @pl.when(sub != ty)
        def _():
            pair_copy(q).wait_recv()

        if nlat > 2:
            @pl.when((sub == ty) & has_from(ty, 2))
            def _():
                far_copy(q, ty).wait_recv()

    def sent(q, ty):
        @pl.when(has_to(ty, 1))
        def _():
            side_copy(q, ty).wait_send()

        @pl.when(sub == ty)
        def _():
            pair_copy(q).wait_send()

        if nlat > 2:
            @pl.when((sub != ty) & has_to(ty, 2))
            def _():
                far_copy(q, ty).wait_send()

        @pl.when(has_from(ty, 1))
        def _():
            hand_copy(q, ty).wait_send()

    send_own(0, 0)
    send_own(1, 1)

    def prepare(i, carry):
        chunk = sea * spec_ref[pl.ds(pl.multiple_of(i * size, size), size), :]
        own_ref[i + 2] = chunk.astype(BF16)
        send_own(i + 2, kind(i + 2))
        return carry

    lax.fori_loop(0, chunks, prepare, 0)

    give_w = pltpu.make_async_remote_copy(
        src_ref=op_ref, dst_ref=w_ref.at[own_half], send_sem=w_send, recv_sem=w_recv,
        device_id=partner, device_id_type=MESH)
    give_w.start()

    for q in (0, 1):
        hand_on(q, q)
    ahead = min(6, chunks)
    for q in range(2, 2 + ahead):
        hand_on(q, kind(q))

    for ty in (0, 1):
        arrive(ty, ty)
        for slot in range(SLOTS):
            row = slot % 2 if ty == 0 else 1 - slot % 2
            cols = slice(row * NLON, (row + 1) * NLON)
            if slot < 6:
                part = halo_ref[2 - slot // 2, ty, :, cols].astype(F32)
            else:
                part = own_ref[ty, :, cols].astype(F32)
            for k, source in enumerate((0, 1, 2 + ty, 4)):
                code_ref[ty, slot, k] = jnp.broadcast_to(part[source:source + 1, :], (8, NLON))

    def propagate(i):
        q = i + 2
        ty = kind(q)

        @pl.when(i + ahead < chunks)
        def _():
            hand_on(q + ahead, kind(q + ahead))

        arrive(q, ty)
        bin0 = first + i * size
        freq = lax.div(bin0, ND)
        direction = lax.rem(bin0, ND)
        to_east = jnp.where((direction < ND // 4) | (direction >= 3 * ND // 4), 1, 0)
        steps = steps_ref[freq]
        speed = cour_ref[freq]
        sign = jnp.where(to_east == 1, 1.0, -1.0)
        shift1 = jnp.where(to_east == 1, 1, NLON - 1)
        shift2 = jnp.where(to_east == 1, 2, NLON - 2)
        back1 = NLON - shift1
        d8 = lax.div(direction, 8)
        abs_cos = cos_ref[pl.ds(d8, planes)]
        abs_sin = sin_ref[pl.ds(d8, planes)]

        def lanes(slot):
            row = jnp.where(ty == 0, slot % 2, 1 - slot % 2)
            return pl.ds(pl.multiple_of(row * NLON, NLON), NLON)

        values = []
        for slot in range(SLOTS):
            if slot < 6:
                part = halo_ref[2 - slot // 2, q, :, lanes(slot)].astype(F32)
            else:
                part = spec_ref[pl.ds(pl.multiple_of(i * size, size), size), lanes(slot)]
            part = part.reshape(planes, 8, NLON)
            if slot >= 6:
                part = part * code_ref[ty, slot, 3][None]
            values.append(part)
        for t in range(MAXSTEPS):
            live = jnp.where(t < steps, speed, 0.0)
            wx = live * abs_cos
            wy = live * abs_sin
            keep = 1.0 - wx - wy
            fresh = list(values)
            for slot in range(t + 1, SLOTS):
                x = values[slot]
                below = values[slot - 1]
                near = code_ref[ty, slot, 1 - to_east][None] == 1.0
                vert = code_ref[ty, slot, 2][None] * sign
                lon = jnp.where(near, pltpu.roll(x, shift1, 2), pltpu.roll(x, shift2, 2))
                up = jnp.where(vert == -1.0, pltpu.roll(below, shift1, 2),
                               jnp.where(vert == 1.0, pltpu.roll(below, back1, 2), below))
                up = jnp.where(jnp.abs(vert) == 2.0, x, up)
                fresh[slot] = code_ref[ty, slot, 3][None] * (keep * x + wx * lon + wy * up)
            values = fresh
        for slot in (6, 7):
            prop_ref[i, :, lanes(slot)] = values[slot].reshape(size, NLON)
        whole = prop_ref[i]
        for c in range(ncomp):
            away_ref[c, i] = whole[:, c * share:(c + 1) * share].astype(BF16)

    groups = chunks // group

    def out_copy(j, g):
        to = lax.rem(me + j, ncomp)
        span = pl.ds(g * group, group)
        return pltpu.make_async_remote_copy(
            src_ref=away_ref.at[to, span], dst_ref=got_ref.at[me, span],
            send_sem=a_send.at[j], recv_sem=a_recv.at[j],
            device_id={"comp": to}, device_id_type=MESH)

    def whole_copy(j):
        to = lax.rem(me + j, ncomp)
        return pltpu.make_async_remote_copy(
            src_ref=away_ref.at[to], dst_ref=got_ref.at[me],
            send_sem=a_send.at[j], recv_sem=a_recv.at[j],
            device_id={"comp": to}, device_id_type=MESH)

    def run_group(g, carry):
        def one(i, inner):
            propagate(g * group + i)
            return inner

        lax.fori_loop(0, group, one, 0)
        for j in range(1, ncomp):
            out_copy(j, g).start()
        return carry

    lax.fori_loop(0, groups, run_group, 0)

    for q in (0, 1):
        sent(q, q)

    def drain(q, carry):
        sent(q, kind(q))
        return carry

    lax.fori_loop(2, chunks + 2, drain, 0)
    got_ref[me] = away_ref[me]
    load_w.wait()
    give_w.wait()

    for j in range(1, ncomp):
        whole_copy(j).wait()
    for c in range(ncomp):
        start_ref[c * bins:(c + 1) * bins, :] = got_ref[c].astype(F32).reshape(bins, share)
    tile = total // TILES
    per_tile = bins // tile if bins >= tile else tile // bins
    for m in range(TILES):
        span = slice(m * tile, (m + 1) * tile)
        low_ref[0, span, :] = start_ref[span, :].astype(BF16)

    def tile_rows(m):
        return pl.ds(pl.multiple_of(m * tile, 16), tile)

    def advance(step, m):
        span = tile_rows(m)
        driving = jnp.dot(w_ref[span, :], low_ref[step % 2], preferred_element_type=F32)
        now = start_ref[span, :] if step == 0 else state_ref[span, :]
        return span, now + STEP_SIZE * now * driving

    for step in range(SRC_STEPS - 1):
        def one_tile(m, carry, step=step):
            span, now = advance(step, m)
            state_ref[span, :] = now
            low_ref[(step + 1) % 2, span, :] = now.astype(BF16)
            return carry

        lax.fori_loop(0, TILES, one_tile, 0)

    def home_copy(j, to):
        return pltpu.make_async_remote_copy(
            src_ref=inc_ref.at[to], dst_ref=home_ref.at[me],
            send_sem=b_send.at[j], recv_sem=b_recv.at[j],
            device_id={"comp": to}, device_id_type=MESH)

    mine = lax.div(me * TILES, ncomp)

    def last_tile(i, carry):
        m = lax.rem(mine + 1 + i, TILES)
        span, now = advance(SRC_STEPS - 1, m)
        gain = now - start_ref[span, :]
        for k in range(per_tile):
            to = m * per_tile + k
            inc_ref[to] = gain[k * bins:(k + 1) * bins, :].astype(BF16)
            j = lax.rem(to - me + ncomp, ncomp)

            @pl.when(to != me)
            def _():
                home_copy(j, to).start()

        return carry

    lax.fori_loop(0, TILES, last_tile, 0)
    home_ref[me] = inc_ref[me]
    for c in range(ncomp):
        j = lax.rem(me - c + ncomp, ncomp)

        @pl.when(me != c)
        def _():
            home_copy(j, lax.rem(me + j, ncomp)).wait()

        cols = slice(c * share, (c + 1) * share)
        before = prop_ref[:, :, cols].reshape(bins, share)
        out_ref[:, cols] = sea[:, cols] * (before + home_ref[c].astype(F32))


def solution(mesh):
    nlat, ncomp = mesh.shape["lat"], mesh.shape["comp"]

    def per_device(spectrum, sea_mask, neighbours, substeps, courant, source_operator):
        bins, points = spectrum.shape
        size = 16 if bins % 16 == 0 else 8
        chunks = bins // size
        group = 5 if chunks % 5 == 0 else 1
        share = points // ncomp
        total = bins * ncomp
        angles = (np.arange(ND, dtype=np.float32) + np.float32(0.5)) * np.float32(2.0 * math.pi / ND)
        spread = lambda v: jnp.asarray(
            np.broadcast_to(np.abs(v).astype(np.float32)[:, None], (ND, NLON)).reshape(ND // 8, 8, NLON))
        vmem = pl.BlockSpec(memory_space=pltpu.VMEM)
        smem = pl.BlockSpec(memory_space=pltpu.SMEM)
        kinds = 3 if nlat == 2 else 4
        return pl.pallas_call(
            functools.partial(kernel, nlat, ncomp, group),
            out_shape=jax.ShapeDtypeStruct((bins, points), F32),
            in_specs=[vmem, vmem, vmem, smem, smem, vmem, vmem, pl.BlockSpec(memory_space=pl.ANY)],
            out_specs=vmem,
            scratch_shapes=[
                pltpu.VMEM((total, total), BF16),
                pltpu.VMEM((chunks + 2, size, points), BF16),
                pltpu.VMEM((3, chunks + 2, size, points), BF16),
                pltpu.VMEM((2, SLOTS, 4, 8, NLON), F32),
                pltpu.VMEM((chunks, size, points), F32),
                pltpu.VMEM((ncomp, chunks, size, share), BF16),
                pltpu.VMEM((ncomp, chunks, size, share), BF16),
                pltpu.VMEM((total, share), F32),
                pltpu.VMEM((total, share), F32),
                pltpu.VMEM((2, total, share), BF16),
                pltpu.VMEM((ncomp, bins, share), BF16),
                pltpu.VMEM((ncomp, bins, share), BF16),
                pltpu.SemaphoreType.DMA((kinds, chunks + 2)),
                pltpu.SemaphoreType.DMA((kinds, chunks + 2)),
                pltpu.SemaphoreType.DMA,
                pltpu.SemaphoreType.DMA,
                pltpu.SemaphoreType.DMA,
                pltpu.SemaphoreType.DMA((ncomp,)),
                pltpu.SemaphoreType.DMA((ncomp,)),
                pltpu.SemaphoreType.DMA((ncomp,)),
                pltpu.SemaphoreType.DMA((ncomp,)),
            ],
            compiler_params=pltpu.CompilerParams(
                collective_id=0, has_side_effects=True, vmem_limit_bytes=56 * 1024 * 1024),
        )(spectrum, sea_mask.reshape(1, points), neighbours, substeps, courant,
          spread(np.cos(angles)), spread(np.sin(angles)), source_operator)

    placed = (
        P("comp", ("members", "lat", "sub")),
        P(("members", "lat", "sub")),
        P(None, ("members", "lat", "sub")),
        P(),
        P(),
        P("sub", None),
    )
    return jax.shard_map(
        per_device,
        mesh=mesh,
        in_specs=placed,
        out_specs=P("comp", ("members", "lat", "sub")),
        check_vma=False,
    )
```

time: 159 us -> 64.6 us (0.41)
  the two profiles are of different devices: /device:TPU:2 before, /device:TPU:0 now
where the time goes in v1:
time: 64.6 us; the launch traced here: 64.4 us
  Pallas kernels  59.4 us (92%)
  local copies, waits for them, and re-layouts  4.99 us (8%)
    pallas_call x1, Pallas kernels, per_device(): pl.pallas_call(functools.partial(kernel, nlat, ncomp, group), out_shape=j...  59.4 us
    another operation x2, local copies, waits for them, and re-layouts  2.78 us
    unnamed x1, local copies, waits for them, and re-layouts  2.21 us

profile of v1, /device:TPU:0, one launch (start us, length us, event | category | flops | bytes accessed | tf_op | source)
XLA Modules:
  0.0 64.4 jit_solution(2125192857612470837)
XLA Ops:
  0.0 1.4 %jit_solution_.6.cos_ref = f32[8,8,256]{2,1,0:T(8,128)} broadcast(f32[8,8]{1,0:T(8,128)} %constant.4.clone), dimensions={0,1} | broadcast | bytes 65792 | tf_op jit(solution)
  1.4 1.4 %jit_solution_.7.sin_ref = f32[8,8,256]{2,1,0:T(8,128)} broadcast(f32[8,8]{1,0:T(8,128)} %constant.5.clone), dimensions={0,1} | broadcast | bytes 65792 | tf_op jit(solution)
  2.8 59.4 %shard_map.82 = f32[480,512]{1,0:T(8,128)} custom-call(f32[480,512]{1,0:T(8,128)} %spec_ref.1, s32[1,512]{1,0:T(1,128)} %bitcast.1, s32[4,512]{1,0:T(4,128)} %nb_ref.1, s32[30]{0:T(128)} %steps_ref.1, f32[30]{0:T(128)} %cour_ref.1, f32[8,8,256]{2,1,0:T(8,128)} %jit_solution_.6.cos_ref, f32[8,8,256]{2,1,0:T(8,128)} %jit_solution_.7.sin_ref, ...), custom_call_target="tpu_custom_call" | custom-call | tf_op jit(solution)/shard_map/pallas_call | solution.py:383
  62.2 2.2 %copy.10 = f32[480,512]{1,0:T(8,128)} copy(f32[480,512]{1,0:T(8,128)} %shard_map.82) | data formatting | bytes 1966080
